TPU v7x, 16 devices: a whole 2x2x2 slice. The times are simulated.
16 devices in a mesh: tp: 2 (over z), dp: 8 (over y, x, core).
Axes of the slice: x: 2, y: 2, z: 2, core: 2. Of those that a mesh axis runs over, the one named last changes fastest.
Arguments:
- design: float32 [131072, 1024], P('dp', 'tp')
- target: float32 [131072], P('dp')
- ridge: float32 [], replicated
Outputs:
- output 1: float32 [1024], replicated
- output 2: float32 [131072], P('dp')
All inputs are finite; a program needn't handle non-finite values.
Results may differ from a plain program's by a relative error of at most 0.001.
Values sent between devices are 32-bit elements.
A program may use at most 1 GiB of HBM per device.

v0:
```python
import jax
import jax.numpy as jnp
from jax import lax
from jax.sharding import PartitionSpec as P

HIGHEST = lax.Precision.HIGHEST
CONTRACT_ROWS = (((0,), (0,)), ((), ()))


def solve_factored(chol_low, rhs_vec):
    half_solve = lax.linalg.triangular_solve(chol_low, rhs_vec[:, None], left_side=True, lower=True)
    return lax.linalg.triangular_solve(chol_low, half_solve, left_side=True, lower=True, transpose_a=True)[:, 0]


def solution(mesh):
    col_ways = mesh.shape['tp']

    def local_fit(design_blk, target_blk, ridge):
        rows_dev, cols_dev = design_blk.shape
        features = cols_dev * col_ways
        sub_rows = rows_dev // col_ways
        col_index = lax.axis_index('tp')
        row_panel = lax.all_to_all(design_blk, 'tp', 0, 1, tiled=True)
        target_part = lax.dynamic_slice_in_dim(target_blk, col_index * sub_rows, sub_rows)
        gram_part = lax.dot_general(row_panel, row_panel, CONTRACT_ROWS, precision=HIGHEST, preferred_element_type=jnp.float32)
        moment_part = lax.dot_general(row_panel, target_part, CONTRACT_ROWS, precision=HIGHEST, preferred_element_type=jnp.float32)
        gram_mat = lax.psum(gram_part, ('tp', 'dp'))
        moment_vec = lax.psum(moment_part, ('tp', 'dp'))
        chol_low = jnp.linalg.cholesky(gram_mat + ridge * jnp.eye(features, dtype=jnp.float32))
        coeffs = solve_factored(chol_low, moment_vec)
        coeff_blk = lax.dynamic_slice_in_dim(coeffs, col_index * cols_dev, cols_dev)
        part_fit = jnp.dot(design_blk, coeff_blk, precision=HIGHEST, preferred_element_type=jnp.float32)
        fitted = lax.psum(part_fit, 'tp')
        return coeffs, target_blk - fitted

    return jax.shard_map(local_fit, mesh=mesh, in_specs=(P('dp', 'tp'), P('dp'), P()), out_specs=(P(), P('dp')), check_vma=False)
```

profile of v0, /device:TPU:0, one launch (start us, length us, event | category | flops | bytes accessed | tf_op | source)
XLA Modules:
  0.0 1039.2 jit_solution(13226262265922196351)
XLA Ops:
  7.2 395.8 %all_to_all.19 = f32[2,8192,512]{2,1,0:T(8,128)} all-to-all(f32[2,8192,512]{2,1,0:T(8,128)} %bitcast.332), channel_id=1, replica_groups=mesh['tp'=2,'dp'=8] {'tp'}, dimensions={0} | all-to-all | bytes 67108864 | tf_op jit(solution)/shard_map/all_to_all | solution.py:23
  403.0 31.1 %copy.41 = f32[8192,2,512]{0,2,1:T(8,128)} copy(f32[8192,2,512]{2,0,1:T(8,128)} %bitcast.333) | data formatting | bytes 67108864 | tf_op jit(solution)/shard_map/all_to_all | solution.py:23
  434.1 117.3 %fusion.121 = f32[1024,1024]{0,1:T(8,128)} fusion(f32[8192,1024]{0,1:T(8,128)} %bitcast.330), kind=kOutput, calls=%fused_computation.249 | convolution fusion | flops 103079215104 | bytes 37748736 | tf_op jit(solution)/shard_map/dot_general | solution.py:25
  552.2 30.7 %fusion.122 = f32[1,1024]{1,0:T(1,128)S(1)} fusion(f32[8192,1]{0,1:T(1,128)S(1)} %bitcast.335, f32[8192,1024]{0,1:T(8,128)} %bitcast.331), kind=kOutput, calls=%fused_computation.250 | convolution fusion | flops 100663296 | bytes 33591296 | tf_op jit(solution)/shard_map/dot_general | solution.py:26
  583.0 32.4 %psum.22 = f32[1024]{0:T(1024)S(1)} all-reduce(f32[1024]{0:T(1024)S(1)} %bitcast.339), channel_id=1, replica_groups=mesh['tp'=2,'dp'=8] {'tp','dp'}, use_global_device_ids=true, to_apply=%region_17.18 | all-reduce | flops 1024 | bytes 8192 | tf_op jit(solution)/shard_map/psum | solution.py:28
  615.3 15.5 %all-reduce.4.cloned.1.call-done = f32[1024,1024]{0,1:T(8,128)} async-done(((f32[1024,1024]{0,1:T(8,128)}), f32[1024,1024]{0,1:T(8,128)}) %all-reduce.4.cloned.1.call-update) | async-done | bytes 4194320 | tf_op jit(solution)/shard_map/psum | solution.py:27
  630.8 4.8 select_add_fusion
  635.6 5.5 copy.43
  641.1 4.5 fusion
  645.6 1.9 copy-done.1
  647.5 11.7 %cholesky.222 = f32[128,128]{1,0:T(8,128)S(1)} custom-call(f32[128,128]{1,0:T(8,128)S(1)} %cholesky.577), custom_call_target="Cholesky" | custom-call | tf_op jit(solution)/shard_map/jit(cholesky)/cholesky | solution.py:29
  659.3 9.8 custom-call.64
  669.1 1.5 fusion.38
  670.6 1.5 convolution_subtract_fusion
  672.5 11.7 %cholesky.243 = f32[128,128]{1,0:T(8,128)S(1)} custom-call(f32[128,128]{1,0:T(8,128)S(1)} %cholesky.581), custom_call_target="Cholesky" | custom-call | tf_op jit(solution)/shard_map/jit(cholesky)/cholesky | solution.py:29
  684.5 9.8 custom-call.65
  695.5 2.0 copy-done
  697.5 2.4 convolution_subtract_fusion.1
  699.9 11.7 %cholesky.466 = f32[128,128]{1,0:T(8,128)S(1)} custom-call(f32[128,128]{1,0:T(8,128)S(1)} %cholesky.586), custom_call_target="Cholesky" | custom-call | tf_op jit(solution)/shard_map/jit(cholesky)/cholesky | solution.py:29
  712.4 9.8 custom-call.66
  722.2 1.3 convolution_dynamic-update-slice_fusion.1
  723.4 3.5 convolution_subtract_fusion.2
  727.0 11.7 %cholesky.485 = f32[128,128]{1,0:T(8,128)S(1)} custom-call(f32[128,128]{1,0:T(8,128)S(1)} %cholesky.591), custom_call_target="Cholesky" | custom-call | tf_op jit(solution)/shard_map/jit(cholesky)/cholesky | solution.py:29
  739.5 9.8 custom-call.67
  749.3 1.1 convolution_dynamic-update-slice_fusion.2
  750.4 3.2 convolution_subtract_fusion.3
  753.6 11.9 %cholesky.504 = f32[128,128]{1,0:T(8,128)S(1)} custom-call(f32[128,128]{1,0:T(8,128)S(1)} %cholesky.596), custom_call_target="Cholesky" | custom-call | tf_op jit(solution)/shard_map/jit(cholesky)/cholesky | solution.py:29
  766.2 9.8 custom-call.68
  776.0 1.1 convolution_dynamic-update-slice_fusion.3
  777.2 3.1 convolution_subtract_fusion.4
  780.3 11.7 %cholesky.524 = f32[128,128]{1,0:T(8,128)S(1)} custom-call(f32[128,128]{1,0:T(8,128)S(1)} %cholesky.601), custom_call_target="Cholesky" | custom-call | tf_op jit(solution)/shard_map/jit(cholesky)/cholesky | solution.py:29
  792.7 9.8 custom-call.69
  803.5 2.9 convolution_subtract_fusion.5
  806.4 11.7 %cholesky.544 = f32[128,128]{1,0:T(8,128)S(1)} custom-call(f32[128,128]{1,0:T(8,128)S(1)} %cholesky.606), custom_call_target="Cholesky" | custom-call | tf_op jit(solution)/shard_map/jit(cholesky)/cholesky | solution.py:29
  818.9 9.8 custom-call.70
  829.7 2.1 convolution_subtract_fusion.6
  831.8 11.7 %cholesky.562 = f32[128,128]{1,0:T(8,128)S(1)} custom-call(f32[128,128]{1,0:T(8,128)S(1)} %convolution_subtract_fusion.6), custom_call_target="Cholesky" | custom-call | tf_op jit(solution)/shard_map/jit(cholesky)/cholesky | solution.py:29
  853.9 4.8 select_select_fusion
  858.7 23.9 %while.1 = (s32[]{:T(128)}, f32[1024,1024]{0,1:T(8,128)}, s32[8,2]{0,1:T(2,128)S(1)}, f32[8,128,128]{2,1,0:T(8,128)S(1)}, s32[]{:T(128)}) while((s32[]{:T(128)}, f32[1024,1024]{0,1:T(8,128)}, s32[8,2]{0,1:T(2,128)S(1)}, f32[8,128,128]{2,1,0:T(8,128)S(1)}, s32[]{:T(128)}) %tuple.55), condition=%wide.while_cond, body=%wide.while_body.sunk | while | flops 2 | bytes 393321 | solution.py:12
  859.3 2.3 dynamic-slice.8
  862.3 2.3 dynamic-slice.8
  865.3 2.3 dynamic-slice.8
  868.3 2.3 dynamic-slice.8
  871.3 2.3 dynamic-slice.8
  874.3 2.3 dynamic-slice.8
  877.3 2.3 dynamic-slice.8
  880.3 2.2 dynamic-slice.8
  882.6 79.0 %custom-call.71 = f32[8,128,128]{1,2,0:T(8,128)S(1)} custom-call(f32[8,128,128]{2,1,0:T(8,128)S(1)} %get-tuple-element.9), custom_call_target="InvertDiagBlocksLowerTriangular" | custom-call | tf_op jit(solution)/shard_map/triangular_solve | solution.py:12
  962.9 1.1 fusion.10
  964.2 1.2 fusion.29
  965.5 1.2 fusion.15
  966.9 1.3 fusion.27
  968.4 1.3 fusion.17
  969.9 1.4 fusion.11
  971.7 1.1 fusion.5
  972.9 1.1 fusion.12
  974.3 1.2 fusion.25
  975.8 1.3 fusion.19
  977.4 1.4 fusion.23
  979.0 1.4 fusion.21
  980.7 1.5 fusion.13
  982.6 31.5 %fusion.92 = f32[1,16384]{1,0:T(1,128)} fusion(f32[16384,512]{1,0:T(8,128)} %param.3, f32[1024,1]{0,1:T(1,128)S(1)} %constant_dynamic-update-slice_fusion.36, s32[]{:T(128)S(6)} %select_n.12), kind=kOutput, calls=%fused_computation.203 | convolution fusion | flops 100663296 | bytes 33622020 | tf_op jit(solution)/shard_map/dot_general | solution.py:32
  1014.1 16.7 %all-reduce.6.cloned.1.call-done = f32[16384]{0:T(1024)} async-done(((f32[16384]{0:T(1024)}), f32[16384]{0:T(1024)}) %all-reduce.6.cloned.1.call-update) | async-done | bytes 65552 | tf_op jit(solution)/shard_map/psum | solution.py:33
  1030.8 1.5 sub.3
  (128 shorter events, 23.2 us)
Async XLA Ops:
  7.2 623.6 %all-reduce.4.cloned.1.call-start = ((), (), s32[]{:S(2)}) async-start(), calls=%async_computation.1 | async-start | bytes 8388608 | tf_op jit(solution)/shard_map/psum | solution.py:27
  551.4 0.8 copy-start.2
  551.4 479.4 %all-reduce.6.cloned.1.call-start = ((), (), s32[]{:S(2)}) async-start(), calls=%async_computation.2 | async-start | bytes 131072 | tf_op jit(solution)/shard_map/psum | solution.py:33
  645.6 1.9 copy-start.1
  695.5 2.0 copy-start
  982.6 31.5 %copy-start.3 = (f32[1024,1]{0,1:T(1,128)}, f32[1024,1]{0,1:T(1,128)S(1)}, u32[]{:S(2)}) copy-start(f32[1024,1]{0,1:T(1,128)S(1)} %constant_dynamic-update-slice_fusion.36) | copy-start | bytes 12292
Sparse Core Ops, SparseCore 0:
  551.5 79.2 all-reduce.3
  1014.2 16.5 all-reduce.5
where the time goes:
time: 1050 us; the launch traced here: 1040 us
  blocking collectives  428 us (41%)
  other arithmetic  262 us (25%)
  matrix products  226 us (22%)
  local copies, waits for them, and re-layouts  70.1 us (7%)
  waiting for transfers between devices  32.2 us (3%)
  between operations  20.2 us (2%)
    all_to_all x1, blocking collectives, local_fit(): row_panel = lax.all_to_all(design_blk, 'tp', 0, 1, tiled=True)  396 us
    another operation x30, other arithmetic, local_fit(): jnp.linalg.cholesky(gram_mat + ridge * jnp.eye(features, dtype=jnp.float32))  167 us
    dot_general x1, matrix products, local_fit(): lax.dot_general(row_panel, row_panel, CONTRACT_ROWS, precision=HIGHEST, p...  117 us
    another operation x3, other arithmetic, solve_factored(): lax.linalg.triangular_solve(chol_low, half_solve, left_side=True, lower=T...  83.8 us
    psum x1, blocking collectives, local_fit(): moment_vec = lax.psum(moment_part, ('tp', 'dp'))  32.4 us
    dot_general x1, matrix products, local_fit(): jnp.dot(design_blk, coeff_blk, precision=HIGHEST, preferred_element_type=...  31.5 us
    all_to_all x1, local copies, waits for them, and re-layouts, local_fit(): row_panel = lax.all_to_all(design_blk, 'tp', 0, 1, tiled=True)  31.1 us
    dot_general x1, matrix products, local_fit(): lax.dot_general(row_panel, target_part, CONTRACT_ROWS, precision=HIGHEST,...  30.7 us
  transfers between devices with their start and end apart: 2, of which 2 were waited for; matrix products, arithmetic and copies ran while one was open for 3% of the time, Pallas kernels for 0%

commit v1 on v0

v1 whole, which is shorter than its diff:
```python
import functools

import jax
import jax.numpy as jnp
from jax import lax
from jax.experimental import pallas as pl
from jax.experimental.pallas import tpu as pltpu
from jax.sharding import PartitionSpec as P

MESH = pl.DeviceIdType.MESH
HIGHEST = lax.Precision.HIGHEST
F32 = jnp.float32
CH = 128
GROUPS = 8
SLOTS = 3


def dot(a, b, ca, cb):
    return lax.dot_general(a, b, (((ca,), (cb,)), ((), ())), precision=HIGHEST, preferred_element_type=F32)


def iota(shape, dim):
    return lax.broadcasted_iota(jnp.int32, shape, dim)


def chol_inverse(s_ref, w_ref):
    w_ref[...] = jnp.where(iota((CH, CH), 0) == iota((CH, CH), 1), 1.0, 0.0).astype(F32)
    lane, sub = iota((8, CH), 1), iota((8, CH), 0)

    def group(g, carry):
        r0 = pl.multiple_of(g * 8, 8)
        rows = s_ref[pl.ds(r0, 8), :]
        inv = w_ref[pl.ds(r0, 8), :]
        cols = [
            jnp.broadcast_to(jnp.sum(jnp.where(lane == r0 + i, rows, 0.0), axis=1, keepdims=True), (8, CH))
            for i in range(8)
        ]
        for i in range(8):
            piv = jnp.broadcast_to(cols[i][i : i + 1, :], (8, CH))
            scale = lax.rsqrt(piv)
            scale = scale * (1.5 - 0.5 * piv * scale * scale)
            coef = jnp.where(sub > i, cols[i] * scale, 0.0)
            u = jnp.broadcast_to(rows[i : i + 1, :], (8, CH)) * scale
            v = jnp.broadcast_to(inv[i : i + 1, :], (8, CH)) * scale
            rows = jnp.where(sub == i, u, rows - coef * u)
            inv = jnp.where(sub == i, v, inv - coef * v)
            for j in range(i + 1, 8):
                cols[j] = cols[j] - coef * jnp.broadcast_to(coef[j : j + 1, :], (8, CH))
        w_ref[pl.ds(r0, 8), :] = inv
        below = jnp.where(lane >= r0 + 8, rows, 0.0)
        upd = dot(below, jnp.concatenate([rows, inv], axis=1), 0, 0)
        s_ref[...] -= upd[:, :CH]
        w_ref[...] -= upd[:, CH:]
        return carry

    lax.fori_loop(0, CH // 8, group, 0)


def kernel(
    lam_ref, b_ref, a_hbm, x_ref, r_ref,
    a_v, xr, gacc, hacc, drecv, hrecv, gall, hall, cacc, crecv, cg, pan, lp, linv, s0, s1, w0, w1, nbuf, hpos, ybuf, pbuf, prec,
    load_sem, xs_sem, xr_sem, ds_sem, dr_sem, hs_sem, hr_sem, gs_sem, gr_sem, rs_sem, rr_sem, ps_sem, pr_sem,
):
    rows, cols = a_v.shape
    half = rows // 2
    nch = cols // CH
    subs = xr_sem.shape[1]
    srows = half // subs
    nload = load_sem.shape[0]
    lrows = rows // nload
    t = lax.axis_index("tp")
    d = lax.axis_index("dp")
    other = 1 - t

    def peer(off):
        return lax.rem(d + off, GROUPS)

    def remote(src, dst, ssem, rsem, tp, dp):
        return pltpu.make_async_remote_copy(
            src_ref=src, dst_ref=dst, send_sem=ssem, recv_sem=rsem, device_id={"tp": tp, "dp": dp}, device_id_type=MESH
        )

    def load(i):
        sl = pl.ds(pl.multiple_of(i * lrows, lrows), lrows)
        return pltpu.make_async_copy(a_hbm.at[sl, :], a_v.at[sl, :], load_sem.at[i])

    barrier = pltpu.get_barrier_semaphore()
    pl.semaphore_signal(barrier, inc=1, device_id={"tp": other, "dp": d}, device_id_type=MESH)
    for off in range(1, GROUPS):
        pl.semaphore_signal(barrier, inc=1, device_id={"tp": t, "dp": peer(off)}, device_id_type=MESH)
    for i in range(nload):
        load(i).start()
    pl.semaphore_wait(barrier, GROUPS)

    def exchange(q):
        c, s = q // subs, q % subs
        src = a_hbm.at[pl.ds(pl.multiple_of(other * half + s * srows, srows), srows), pl.ds(c * CH, CH)]
        return remote(src, xr.at[c % SLOTS, pl.ds(s * srows, srows), :], xs_sem.at[c, s], xr_sem.at[c, s], other, d)

    def issue(lo, hi):
        for q in range(lo, hi):
            exchange(q).start()

    total = nch * subs
    ahead = [subs + 3] + [min((k + 2) * subs + 2, total) for k in range(nch)]
    issue(0, ahead[0])

    gacc[...] = jnp.zeros_like(gacc)
    hacc[...] = jnp.zeros_like(hacc)
    pan[...] = jnp.zeros_like(pan)
    lp[...] = jnp.zeros_like(lp)
    linv[...] = jnp.zeros_like(linv)
    ybuf[...] = jnp.zeros_like(ybuf)
    eye = iota((CH, CH), 0) == iota((CH, CH), 1)

    mid = cols // 2

    def diag(i, carry):
        load(i).wait()
        sl = pl.ds(pl.multiple_of(i * lrows, lrows), lrows)
        gacc[:mid, :] += dot(a_v[sl, :mid], a_v[sl, :], 0, 0)
        gacc[mid:, mid:] += dot(a_v[sl, mid:], a_v[sl, mid:], 0, 0)

        def moment(j, c2):
            g = i * (lrows // CH) + j
            brow = jnp.broadcast_to(b_ref[pl.ds(g, 1), :], (CH, CH))
            bcol = jnp.sum(jnp.where(eye, brow, 0.0), axis=1, keepdims=True)
            blk = a_v[pl.ds(pl.multiple_of(g * CH, CH), CH), :]
            hacc[...] += jnp.sum((blk * bcol).reshape(CH // 8, 8, cols), axis=0)
            return c2

        return lax.fori_loop(0, lrows // CH, moment, carry)

    lax.fori_loop(0, nload, diag, 0)
    gacc[mid:, :mid] = gacc[:mid, mid:].T

    pr = cols // GROUPS

    def rows_of(p, n):
        return pl.ds(pl.multiple_of(p * n, n), n)

    def diag_send(off):
        p = peer(off)
        return remote(gacc.at[rows_of(p, pr), :], drecv.at[off - 1], ds_sem.at[off - 1], dr_sem.at[off - 1], t, p)

    def mom_send(off):
        return remote(hacc, hrecv.at[d], hs_sem.at[off - 1], hr_sem.at[off - 1], t, peer(off))

    def mom_arrive(off):
        src = lax.rem(d + GROUPS - off, GROUPS)
        return remote(hacc, hrecv.at[src], hs_sem.at[off - 1], hr_sem.at[off - 1], t, peer(off))

    for off in range(1, GROUPS):
        diag_send(off).start()
        mom_send(off).start()
    hrecv[d] = hacc[...]

    cr = CH // GROUPS

    def cross(k):
        cacc[...] = jnp.zeros_like(cacc)

        def step(s, carry):
            sl = pl.ds(pl.multiple_of(s * srows, srows), srows)
            buf = xr.at[k % SLOTS, sl, :]
            remote(buf, buf, xs_sem.at[k, s], xr_sem.at[k, s], other, d).wait_recv()
            mine = a_v[pl.ds(pl.multiple_of(t * half + s * srows, srows), srows), :]
            cacc[...] += dot(xr[k % SLOTS, sl, :], mine, 0, 0)
            return carry

        lax.fori_loop(0, subs, step, 0)

    def cross_send(k, off):
        p = peer(off)
        return remote(cacc.at[rows_of(p, cr), :], crecv.at[k, off - 1], rs_sem.at[k, off - 1], rr_sem.at[k, off - 1], t, p)

    def spread(ref, n, ssem, rsem, slot, off):
        if slot == 7:
            return remote(ref.at[t, rows_of(d, n), :], ref.at[t, rows_of(d, n), :], ssem.at[7], rsem.at[7], other, d)
        plane = t if slot < 7 else other
        return remote(
            ref.at[plane, rows_of(d, n), :], ref.at[plane, rows_of(d, n), :], ssem.at[slot], rsem.at[slot], t, peer(off)
        )

    def arrive(ref, n, ssem, rsem, slot, off):
        if slot == 7:
            piece = ref.at[other, rows_of(d, n), :]
            return remote(piece, piece, ssem.at[7], rsem.at[7], other, d)
        src = lax.rem(d + GROUPS - off, GROUPS)
        piece = ref.at[t if slot < 7 else other, rows_of(src, n), :]
        return remote(piece, piece, ssem.at[slot], rsem.at[slot], t, peer(off))

    def gather_start(ref, n, ssem, rsem):
        spread(ref, n, ssem, rsem, 7, 0).start()
        for off in range(1, GROUPS):
            spread(ref, n, ssem, rsem, off - 1, off).start()

    def gather_finish(ref, n, ssem, rsem):
        arrive(ref, n, ssem, rsem, 7, 0).wait_recv()
        for off in range(1, GROUPS):
            spread(ref, n, ssem, rsem, 7 + off, off).start()
        for off in range(1, GROUPS):
            arrive(ref, n, ssem, rsem, off - 1, off).wait_recv()
        for off in range(1, GROUPS):
            arrive(ref, n, ssem, rsem, 7 + off, off).wait_recv()
        for slot in range(7):
            spread(ref, n, ssem, rsem, slot, slot + 1).wait_send()
        spread(ref, n, ssem, rsem, 7, 0).wait_send()
        for off in range(1, GROUPS):
            spread(ref, n, ssem, rsem, 7 + off, off).wait_send()

    def cross_reduce(k):
        for off in range(1, GROUPS):
            cross_send(k, off).start()
        acc = cacc[rows_of(d, cr), :]
        for off in range(1, GROUPS):
            cross_send(k, off).wait_recv()
            acc = acc + crecv[k, off - 1]
        cg[k, t, rows_of(d, cr), :] = acc
        for off in range(1, GROUPS):
            cross_send(k, off).wait_send()

    def diag_reduce():
        acc = gacc[rows_of(d, pr), :]
        for off in range(1, GROUPS):
            diag_send(off).wait_recv()
            acc = acc + drecv[off - 1]
        gall[t, rows_of(d, pr), :] = acc
        for off in range(1, GROUPS):
            mom_arrive(off).wait_recv()
        mom = hrecv[0]
        for p in range(1, GROUPS):
            mom = mom + hrecv[p]
        hall[t] = mom
        for off in range(1, GROUPS):
            diag_send(off).wait_send()
            mom_send(off).wait_send()

    def mom_swap(plane):
        piece = hall.at[plane]
        return remote(piece, piece, hs_sem.at[7], hr_sem.at[7], other, d)

    def factor(k):
        wide = 2 * CH
        for tr in range(2):
            for j in range(k + 1):
                for tc in range(2):
                    if tr == tc:
                        blk = gall[tr, k * CH : (k + 1) * CH, j * CH : (j + 1) * CH]
                    else:
                        blk = cg[k, tc, :, j * CH : (j + 1) * CH] + cg[j, tr, :, k * CH : (k + 1) * CH].T
                    pan[tr * CH : (tr + 1) * CH, j * wide + tc * CH : j * wide + (tc + 1) * CH] = blk
        low = k * wide
        for n in range(k):
            seen = (n + 1) * wide
            lp[:, n * wide : seen] = dot(pan[:, :seen], linv[n * wide : seen, :seen], 1, 1)
        ridge = lam_ref[0, 0]
        sch = pan[:, low : low + wide] + jnp.where(iota((wide, wide), 0) == iota((wide, wide), 1), ridge, 0.0)
        if k:
            sch = sch - dot(lp[:, :low], lp[:, :low], 1, 1)
        s0[...] = sch[:CH, :CH]
        s10 = sch[CH:, :CH]
        chol_inverse(s0, w0)
        n00 = w0[...]
        l10 = dot(s10, n00, 1, 1)
        s1[...] = sch[CH:, CH:] - dot(l10, l10, 1, 1)
        chol_inverse(s1, w1)
        n11 = w1[...]
        nbuf[:CH, :CH] = n00
        nbuf[:CH, CH:] = jnp.zeros((CH, CH), F32)
        nbuf[CH:, :CH] = -dot(n11, dot(l10, n00, 1, 0), 1, 0)
        nbuf[CH:, CH:] = n11
        rhs = hpos[:, low : low + wide]
        if k:
            rhs = rhs - dot(ybuf[:, :low], lp[:, :low], 1, 1)
        y = dot(rhs, nbuf[...], 1, 1)
        if k == nch - 1:
            return y
        ybuf[:, low : low + wide] = y
        for n in range(k):
            sl = slice(n * wide, (n + 1) * wide)
            part = dot(lp[:, n * wide : low], linv[n * wide : low, sl], 1, 0)
            linv[low : low + wide, sl] = -dot(nbuf[...], part, 1, 0)
        linv[low : low + wide, low : low + wide] = nbuf[...]
        return y

    y = None
    for k in range(nch):
        cross(k)
        if k == 0:
            diag_reduce()
            gather_start(gall, pr, gs_sem.at[nch], gr_sem.at[nch])
            mom_swap(t).start()
        cross_reduce(k)
        gather_start(cg.at[k], cr, gs_sem.at[k], gr_sem.at[k])
        issue(ahead[k], ahead[k + 1])
        gather_finish(cg.at[k], cr, gs_sem.at[k], gr_sem.at[k])
        if k == 0:
            gather_finish(gall, pr, gs_sem.at[nch], gr_sem.at[nch])
            mom_swap(other).wait_recv()
            mom_swap(t).wait_send()
            for tt in range(2):
                hrow = jnp.broadcast_to(jnp.sum(hall[tt], axis=0, keepdims=True), (8, cols))
                for j in range(nch):
                    p = (2 * j + tt) * CH
                    hpos[:, p : p + CH] = hrow[:, j * CH : (j + 1) * CH]
        y = factor(k)

    last = dot(y, nbuf[...], 1, 0)
    rest = dot(ybuf[...] - dot(last, lp[...], 1, 0), linv[...], 1, 0)
    xpos = jnp.concatenate([rest, last], axis=1)
    sides = [
        jnp.concatenate([xpos[0:1, (2 * j + tt) * CH : (2 * j + tt + 1) * CH] for j in range(nch)], axis=1) for tt in range(2)
    ]
    for tt in range(2):
        for j in range(nch):
            x_ref[tt * nch + j : tt * nch + j + 1, :] = sides[tt][:, j * CH : (j + 1) * CH]
    own = jnp.where(t == 0, sides[0], sides[1])

    def fit(g, carry):
        blk = a_v[pl.ds(pl.multiple_of(g * CH, CH), CH), :] * own
        tot = blk[:, :CH]
        for j in range(1, nch):
            tot = tot + blk[:, j * CH : (j + 1) * CH]
        tot = jnp.sum(tot, axis=1, keepdims=True)
        pbuf[pl.ds(g, 1), :] = jnp.sum(jnp.where(eye, tot, 0.0), axis=0, keepdims=True)
        return carry

    ngroup = rows // CH
    parts = ps_sem.shape[0]
    per = ngroup // parts

    def swap(q):
        sl = pl.ds(q * per, per)
        return remote(pbuf.at[sl, :], prec.at[sl, :], ps_sem.at[q], pr_sem.at[q], other, d)

    for q in range(parts):
        lax.fori_loop(q * per, (q + 1) * per, fit, 0)
        swap(q).start()
    for q in range(parts):
        swap(q).wait_recv()
        sl = pl.ds(q * per, per)
        r_ref[sl, :] = b_ref[sl, :] - (pbuf[sl, :] + prec[sl, :])
    for q in range(parts):
        swap(q).wait_send()
    for q in range(total):
        exchange(q).wait_send()


def solution(mesh):
    def local_fit(design, target, ridge):
        rows, cols = design.shape
        half = rows // 2
        nch = cols // CH
        subs = 8
        nload = 16
        wide = 2 * CH
        prev = (nch - 1) * wide
        ngroup = rows // CH
        vm = pltpu.VMEM
        dma = pltpu.SemaphoreType.DMA
        scratch = [
            vm((rows, cols), F32),
            vm((SLOTS, half, CH), F32),
            vm((cols, cols), F32),
            vm((8, cols), F32),
            vm((GROUPS - 1, cols // GROUPS, cols), F32),
            vm((GROUPS, 8, cols), F32),
            vm((2, cols, cols), F32),
            vm((2, 8, cols), F32),
            vm((CH, cols), F32),
            vm((nch, GROUPS - 1, CH // GROUPS, cols), F32),
            vm((nch, 2, CH, cols), F32),
            vm((wide, nch * wide), F32),
            vm((wide, prev), F32),
            vm((prev, prev), F32),
            vm((CH, CH), F32),
            vm((CH, CH), F32),
            vm((CH, CH), F32),
            vm((CH, CH), F32),
            vm((wide, wide), F32),
            vm((8, nch * wide), F32),
            vm((8, prev), F32),
            vm((ngroup, CH), F32),
            vm((ngroup, CH), F32),
            dma((nload,)),
            dma((nch, subs)),
            dma((nch, subs)),
            dma((7,)),
            dma((7,)),
            dma((8,)),
            dma((8,)),
            dma((nch + 1, 15)),
            dma((nch + 1, 15)),
            dma((nch, 7)),
            dma((nch, 7)),
            dma((4,)),
            dma((4,)),
        ]
        x, r = pl.pallas_call(
            kernel,
            out_shape=(jax.ShapeDtypeStruct((2 * nch, CH), F32), jax.ShapeDtypeStruct((ngroup, CH), F32)),
            in_specs=[
                pl.BlockSpec(memory_space=pltpu.SMEM),
                pl.BlockSpec(memory_space=pltpu.VMEM),
                pl.BlockSpec(memory_space=pl.ANY),
            ],
            out_specs=(pl.BlockSpec(memory_space=pltpu.VMEM), pl.BlockSpec(memory_space=pltpu.VMEM)),
            scratch_shapes=scratch,
            compiler_params=pltpu.CompilerParams(collective_id=0, has_side_effects=True, vmem_limit_bytes=67043328),
        )(ridge.reshape(1, 1), target.reshape(ngroup, CH), design)
        return x.reshape(-1), r.reshape(-1)

    return jax.shard_map(
        local_fit, mesh=mesh, in_specs=(P("dp", "tp"), P("dp"), P()), out_specs=(P(), P("dp")), check_vma=False
    )
```

time: 1050 us -> 432 us (0.41)
  blocking collectives: 428 us -> 0 us
  Pallas kernels: 0 us -> 427 us
  other arithmetic: 262 us -> 0 us
  matrix products: 226 us -> 0 us
  local copies, waits for them, and re-layouts: 70.1 us -> 2.74 us
  waiting for transfers between devices: 32.2 us -> 0 us
  between operations: 20.2 us -> 1.29 us
    pallas_call x0 -> x1, Pallas kernels: none -> 427 us  [local_fit(): pl.pallas_call(kernel, out_shape=(jax.ShapeDtypeStruct((2 * nch, CH), F32...]
    all_to_all x1 -> x0, blocking collectives: 396 us -> none  [local_fit(): row_panel = lax.all_to_all(design_blk, 'tp', 0, 1, tiled=True)]
    another operation x33 -> x0, other arithmetic: 251 us -> none  [the longest x30 167 us: local_fit(): jnp.linalg.cholesky(gram_mat + ridge * jnp.eye(features, dtype=jnp.float32))]
    dot_general x3 -> x0, matrix products: 179 us -> none  [the longest x1 117 us: local_fit(): lax.dot_general(row_panel, row_panel, CONTRACT_ROWS, precision=HIGHEST, p...]
    another operation x44 -> x0, matrix products: 46.7 us -> none  [the longest x14 26.2 us: local_fit(): jnp.linalg.cholesky(gram_mat + ridge * jnp.eye(features, dtype=jnp.float32))]
    psum x1 -> x0, blocking collectives: 32.4 us -> none  [local_fit(): moment_vec = lax.psum(moment_part, ('tp', 'dp'))]
    psum x2 -> x0, waiting for transfers between devices: 32.2 us -> none  [the longest x1 16.7 us: local_fit(): fitted = lax.psum(part_fit, 'tp')]
    all_to_all x1 -> x0, local copies, waits for them, and re-layouts: 31.1 us -> none  [local_fit(): row_panel = lax.all_to_all(design_blk, 'tp', 0, 1, tiled=True)]
  transfers between devices with their start and end apart: 2 -> 0, of which waited for: 2 -> 0; matrix products, arithmetic and copies ran while one was open for 3% -> 0% of each run, Pallas kernels for 0% -> 0%
where the time goes in v1:
time: 432 us
  Pallas kernels  427 us (99%)
    pallas_call x1, Pallas kernels, local_fit(): pl.pallas_call(kernel, out_shape=(jax.ShapeDtypeStruct((2 * nch, CH), F32...  427 us

profile of v1, /device:TPU:0, one launch (start us, length us, event | category | flops | bytes accessed | tf_op | source)
XLA Modules:
  0.0 431.5 jit_solution(1524398894071905558)
XLA Ops:
  1.3 427.5 %shard_map.50 = (f32[8,128]{1,0:T(8,128)}, f32[128,128]{1,0:T(8,128)}) custom-call(f32[1,1]{1,0:T(1,128)} %bitcast.4.lam_ref, f32[128,128]{1,0:T(8,128)} %bitcast.5, f32[16384,512]{1,0:T(8,128)} %a_hbm.1), custom_call_target="tpu_custom_call" | custom-call | tf_op jit(solution)/shard_map/pallas_call | solution.py:400
  428.8 1.3 copy.8
  430.0 1.5 copy.9

commit v2 on v1

--- a/solution.py
+++ b/solution.py
@@ -12,6 +12,8 @@
 F32 = jnp.float32
 CH = 128
 GROUPS = 8
+STEP = 8
+LAST_STEP = 32
 SLOTS = 3
 
 
@@ -23,43 +25,66 @@
     return lax.broadcasted_iota(jnp.int32, shape, dim)
 
 
-def chol_inverse(s_ref, w_ref):
+def chol_inverse(s_ref, w_ref, step):
     w_ref[...] = jnp.where(iota((CH, CH), 0) == iota((CH, CH), 1), 1.0, 0.0).astype(F32)
     lane, sub = iota((8, CH), 1), iota((8, CH), 0)
+    tiles = step // 8
+
+    def spread(row):
+        return jnp.broadcast_to(row, (8, CH))
 
     def group(g, carry):
-        r0 = pl.multiple_of(g * 8, 8)
-        rows = s_ref[pl.ds(r0, 8), :]
-        inv = w_ref[pl.ds(r0, 8), :]
+        r0 = pl.multiple_of(g * step, step)
+        rows = [s_ref[pl.ds(r0 + 8 * a, 8), :] for a in range(tiles)]
+        inv = [w_ref[pl.ds(r0 + 8 * a, 8), :] for a in range(tiles)]
         cols = [
-            jnp.broadcast_to(jnp.sum(jnp.where(lane == r0 + i, rows, 0.0), axis=1, keepdims=True), (8, CH))
-            for i in range(8)
+            [
+                spread(jnp.sum(jnp.where(lane == r0 + i, rows[a], 0.0), axis=1, keepdims=True)) if a >= i // 8 else None
+                for a in range(tiles)
+            ]
+            for i in range(step)
         ]
-        for i in range(8):
-            piv = jnp.broadcast_to(cols[i][i : i + 1, :], (8, CH))
+        for i in range(step):
+            a0, r = divmod(i, 8)
+            piv = spread(cols[i][a0][r : r + 1, :])
             scale = lax.rsqrt(piv)
             scale = scale * (1.5 - 0.5 * piv * scale * scale)
-            coef = jnp.where(sub > i, cols[i] * scale, 0.0)
-            u = jnp.broadcast_to(rows[i : i + 1, :], (8, CH)) * scale
-            v = jnp.broadcast_to(inv[i : i + 1, :], (8, CH)) * scale
-            rows = jnp.where(sub == i, u, rows - coef * u)
-            inv = jnp.where(sub == i, v, inv - coef * v)
-            for j in range(i + 1, 8):
-                cols[j] = cols[j] - coef * jnp.broadcast_to(coef[j : j + 1, :], (8, CH))
-        w_ref[pl.ds(r0, 8), :] = inv
-        below = jnp.where(lane >= r0 + 8, rows, 0.0)
-        upd = dot(below, jnp.concatenate([rows, inv], axis=1), 0, 0)
-        s_ref[...] -= upd[:, :CH]
-        w_ref[...] -= upd[:, CH:]
+            u = spread(rows[a0][r : r + 1, :]) * scale
+            v = spread(inv[a0][r : r + 1, :]) * scale
+            coef = [None] * tiles
+            for a in range(a0, tiles):
+                c = cols[i][a] * scale
+                coef[a] = jnp.where(sub > r, c, 0.0) if a == a0 else c
+                down, side = rows[a] - coef[a] * u, inv[a] - coef[a] * v
+                rows[a] = jnp.where(sub == r, u, down) if a == a0 else down
+                inv[a] = jnp.where(sub == r, v, side) if a == a0 else side
+            for j in range(i + 1, step):
+                b0, q = divmod(j, 8)
+                lead = spread(coef[b0][q : q + 1, :])
+                for a in range(b0, tiles):
+                    cols[j][a] = cols[j][a] - coef[a] * lead
+        for a in range(tiles):
+            w_ref[pl.ds(r0 + 8 * a, 8), :] = inv[a]
+        panel = jnp.concatenate(rows, axis=0)
+        both = jnp.concatenate([panel, jnp.concatenate(inv, axis=0)], axis=1)
+
+        @pl.when(g < CH // step - 1)
+        def _():
+            below = jnp.where(iota((step, CH), 1) >= r0 + step, panel, 0.0)
+            upd = dot(below, both, 0, 0)
+            s_ref[...] -= upd[:, :CH]
+            w_ref[...] -= upd[:, CH:]
+
         return carry
 
-    lax.fori_loop(0, CH // 8, group, 0)
+    lax.fori_loop(0, CH // step, group, 0)
 
 
 def kernel(
-    lam_ref, b_ref, a_hbm, x_ref, r_ref,
-    a_v, xr, gacc, hacc, drecv, hrecv, gall, hall, cacc, crecv, cg, pan, lp, linv, s0, s1, w0, w1, nbuf, hpos, ybuf, pbuf, prec,
-    load_sem, xs_sem, xr_sem, ds_sem, dr_sem, hs_sem, hr_sem, gs_sem, gr_sem, rs_sem, rr_sem, ps_sem, pr_sem,
+    lam_ref, b_hbm, a_hbm, x_hbm, r_hbm,
+    b_ref, x_ref, r_ref,
+    a_v, xr, gacc, hacc, drecv, hrecv, gall, hall, cacc, crecv, cg, pan, lp, linv, s0, s1, w0, nbuf, hpos, ybuf, pbuf, prec,
+    small_sem, load_sem, xs_sem, xr_sem, ds_sem, dr_sem, hs_sem, hr_sem, gs_sem, gr_sem, rs_sem, rr_sem, ps_sem, pr_sem, out_sem,
 ):
     rows, cols = a_v.shape
     half = rows // 2
@@ -104,6 +129,8 @@
     total = nch * subs
     ahead = [subs + 3] + [min((k + 2) * subs + 2, total) for k in range(nch)]
     issue(0, ahead[0])
+    b_in = pltpu.make_async_copy(b_hbm, b_ref, small_sem.at[0])
+    b_in.start()
 
     gacc[...] = jnp.zeros_like(gacc)
     hacc[...] = jnp.zeros_like(hacc)
@@ -113,6 +140,8 @@
     ybuf[...] = jnp.zeros_like(ybuf)
     eye = iota((CH, CH), 0) == iota((CH, CH), 1)
 
+    b_in.wait()
+
     mid = cols // 2
 
     def diag(i, carry):
@@ -240,16 +269,24 @@
         piece = hall.at[plane]
         return remote(piece, piece, hs_sem.at[7], hr_sem.at[7], other, d)
 
-    def factor(k):
-        wide = 2 * CH
+    wide = 2 * CH
+
+    def pan_at(tr, tc, j):
+        return slice(tr * CH, (tr + 1) * CH), slice(j * wide + tc * CH, j * wide + (tc + 1) * CH)
+
+    def prepare(k):
         for tr in range(2):
             for j in range(k + 1):
-                for tc in range(2):
-                    if tr == tc:
-                        blk = gall[tr, k * CH : (k + 1) * CH, j * CH : (j + 1) * CH]
-                    else:
-                        blk = cg[k, tc, :, j * CH : (j + 1) * CH] + cg[j, tr, :, k * CH : (k + 1) * CH].T
-                    pan[tr * CH : (tr + 1) * CH, j * wide + tc * CH : j * wide + (tc + 1) * CH] = blk
+                pan[pan_at(tr, tr, j)] = gall[tr, k * CH : (k + 1) * CH, j * CH : (j + 1) * CH]
+                if j < k:
+                    pan[pan_at(tr, 1 - tr, j)] = cg[j, tr, :, k * CH : (k + 1) * CH].T
+
+    def factor(k):
+        for tr in range(2):
+            for j in range(k):
+                pan[pan_at(tr, 1 - tr, j)] += cg[k, 1 - tr, :, j * CH : (j + 1) * CH]
+        here = slice(k * CH, (k + 1) * CH)
+        pan[pan_at(1, 0, k)] = cg[k, 0, :, here] + cg[k, 1, :, here].T
         low = k * wide
         for n in range(k):
             seen = (n + 1) * wide
@@ -258,34 +295,41 @@
         sch = pan[:, low : low + wide] + jnp.where(iota((wide, wide), 0) == iota((wide, wide), 1), ridge, 0.0)
         if k:
             sch = sch - dot(lp[:, :low], lp[:, :low], 1, 1)
-        s0[...] = sch[:CH, :CH]
-        s10 = sch[CH:, :CH]
-        chol_inverse(s0, w0)
-        n00 = w0[...]
-        l10 = dot(s10, n00, 1, 1)
-        s1[...] = sch[CH:, CH:] - dot(l10, l10, 1, 1)
-        chol_inverse(s1, w1)
-        n11 = w1[...]
+        s0[0] = sch[:CH, :CH]
+        s1[...] = sch[CH:, :]
+
+        def block(h, carry):
+            @pl.when(h == 1)
+            def _():
+                l10 = dot(s1[:, :CH], w0[0], 1, 1)
+                s0[1] = s1[:, CH:] - dot(l10, l10, 1, 1)
+                s1[:, :CH] = l10
+
+            chol_inverse(s0.at[h], w0.at[h], STEP if k < nch - 1 else LAST_STEP)
+            return carry
+
+        lax.fori_loop(0, 2, block, 0)
+        n00, n11 = w0[0], w0[1]
         nbuf[:CH, :CH] = n00
         nbuf[:CH, CH:] = jnp.zeros((CH, CH), F32)
-        nbuf[CH:, :CH] = -dot(n11, dot(l10, n00, 1, 0), 1, 0)
+        nbuf[CH:, :CH] = -dot(n11, dot(s1[:, :CH], n00, 1, 0), 1, 0)
         nbuf[CH:, CH:] = n11
+        if k == nch - 1:
+            return
         rhs = hpos[:, low : low + wide]
         if k:
             rhs = rhs - dot(ybuf[:, :low], lp[:, :low], 1, 1)
         y = dot(rhs, nbuf[...], 1, 1)
-        if k == nch - 1:
-            return y
         ybuf[:, low : low + wide] = y
         for n in range(k):
             sl = slice(n * wide, (n + 1) * wide)
             part = dot(lp[:, n * wide : low], linv[n * wide : low, sl], 1, 0)
             linv[low : low + wide, sl] = -dot(nbuf[...], part, 1, 0)
         linv[low : low + wide, low : low + wide] = nbuf[...]
-        return y
-
-    y = None
+
     for k in range(nch):
+        if k:
+            prepare(k)
         cross(k)
         if k == 0:
             diag_reduce()
@@ -304,11 +348,32 @@
                 for j in range(nch):
                     p = (2 * j + tt) * CH
                     hpos[:, p : p + CH] = hrow[:, j * CH : (j + 1) * CH]
-        y = factor(k)
-
-    last = dot(y, nbuf[...], 1, 0)
-    rest = dot(ybuf[...] - dot(last, lp[...], 1, 0), linv[...], 1, 0)
-    xpos = jnp.concatenate([rest, last], axis=1)
+            prepare(0)
+        factor(k)
+
+    def to_row(col):
+        n = col.shape[0] // CH
+        return jnp.concatenate(
+            [jnp.sum(jnp.where(eye, col[i * CH : (i + 1) * CH], 0.0), axis=0, keepdims=True) for i in range(n)], axis=1
+        )
+
+    def to_col(row):
+        n = row.shape[1] // CH
+        return jnp.concatenate(
+            [jnp.sum(jnp.where(eye, row[:, i * CH : (i + 1) * CH], 0.0), axis=1, keepdims=True) for i in range(n)], axis=0
+        )
+
+    def down(mat, col):
+        return jnp.sum(mat * col, axis=0, keepdims=True)
+
+    prev = (nch - 1) * wide
+    seen = jnp.sum(lp[...] * ybuf[0:1, :], axis=1, keepdims=True)
+    rhs = hpos[0:1, prev:] - to_row(seen)
+    ycol = jnp.sum(nbuf[...] * rhs, axis=1, keepdims=True)
+    last = down(nbuf[...], ycol)
+    ucol = to_col(ybuf[0:1, :] - down(lp[...], to_col(last)))
+    rest = [down(linv[n * wide :, n * wide : (n + 1) * wide], ucol[n * wide :]) for n in range(nch - 1)]
+    xpos = jnp.concatenate(rest + [last], axis=1)
     sides = [
         jnp.concatenate([xpos[0:1, (2 * j + tt) * CH : (2 * j + tt + 1) * CH] for j in range(nch)], axis=1) for tt in range(2)
     ]
@@ -316,14 +381,17 @@
         for j in range(nch):
             x_ref[tt * nch + j : tt * nch + j + 1, :] = sides[tt][:, j * CH : (j + 1) * CH]
     own = jnp.where(t == 0, sides[0], sides[1])
-
-    def fit(g, carry):
-        blk = a_v[pl.ds(pl.multiple_of(g * CH, CH), CH), :] * own
-        tot = blk[:, :CH]
-        for j in range(1, nch):
-            tot = tot + blk[:, j * CH : (j + 1) * CH]
-        tot = jnp.sum(tot, axis=1, keepdims=True)
-        pbuf[pl.ds(g, 1), :] = jnp.sum(jnp.where(eye, tot, 0.0), axis=0, keepdims=True)
+    x_out = pltpu.make_async_copy(x_ref, x_hbm, small_sem.at[1])
+    x_out.start()
+
+    def fit(m, carry):
+        for g in range(8):
+            blk = a_v[pl.ds(pl.multiple_of((m * 8 + g) * CH, CH), CH), :] * own
+            tot = blk[:, :CH]
+            for j in range(1, nch):
+                tot = tot + blk[:, j * CH : (j + 1) * CH]
+            tot = jnp.sum(tot, axis=1, keepdims=True)
+            pbuf[pl.ds(m * 8 + g, 1), :] = jnp.sum(jnp.where(eye, tot, 0.0), axis=0, keepdims=True)
         return carry
 
     ngroup = rows // CH
@@ -334,17 +402,25 @@
         sl = pl.ds(q * per, per)
         return remote(pbuf.at[sl, :], prec.at[sl, :], ps_sem.at[q], pr_sem.at[q], other, d)
 
+    def r_out(q):
+        sl = pl.ds(q * per, per)
+        return pltpu.make_async_copy(r_ref.at[sl, :], r_hbm.at[sl, :], out_sem.at[q])
+
     for q in range(parts):
-        lax.fori_loop(q * per, (q + 1) * per, fit, 0)
+        lax.fori_loop(q * per // 8, (q + 1) * per // 8, fit, 0)
         swap(q).start()
     for q in range(parts):
         swap(q).wait_recv()
         sl = pl.ds(q * per, per)
         r_ref[sl, :] = b_ref[sl, :] - (pbuf[sl, :] + prec[sl, :])
+        r_out(q).start()
     for q in range(parts):
         swap(q).wait_send()
     for q in range(total):
         exchange(q).wait_send()
+    x_out.wait()
+    for q in range(parts):
+        r_out(q).wait()
 
 
 def solution(mesh):
@@ -360,6 +436,9 @@
         vm = pltpu.VMEM
         dma = pltpu.SemaphoreType.DMA
         scratch = [
+            vm((ngroup, CH), F32),
+            vm((2 * nch, CH), F32),
+            vm((ngroup, CH), F32),
             vm((rows, cols), F32),
             vm((SLOTS, half, CH), F32),
             vm((cols, cols), F32),
@@ -374,15 +453,15 @@
             vm((wide, nch * wide), F32),
             vm((wide, prev), F32),
             vm((prev, prev), F32),
-            vm((CH, CH), F32),
-            vm((CH, CH), F32),
-            vm((CH, CH), F32),
-            vm((CH, CH), F32),
+            vm((2, CH, CH), F32),
+            vm((CH, wide), F32),
+            vm((2, CH, CH), F32),
             vm((wide, wide), F32),
             vm((8, nch * wide), F32),
             vm((8, prev), F32),
             vm((ngroup, CH), F32),
             vm((ngroup, CH), F32),
+            dma((2,)),
             dma((nload,)),
             dma((nch, subs)),
             dma((nch, subs)),
@@ -396,19 +475,24 @@
             dma((nch, 7)),
             dma((4,)),
             dma((4,)),
+            dma((4,)),
         ]
         x, r = pl.pallas_call(
             kernel,
             out_shape=(jax.ShapeDtypeStruct((2 * nch, CH), F32), jax.ShapeDtypeStruct((ngroup, CH), F32)),
-            in_specs=[
-                pl.BlockSpec(memory_space=pltpu.SMEM),
-                pl.BlockSpec(memory_space=pltpu.VMEM),
-                pl.BlockSpec(memory_space=pl.ANY),
-            ],
-            out_specs=(pl.BlockSpec(memory_space=pltpu.VMEM), pl.BlockSpec(memory_space=pltpu.VMEM)),
+            in_specs=[pl.BlockSpec(memory_space=pltpu.SMEM)] + [pl.BlockSpec(memory_space=pl.ANY)] * 2,
+            out_specs=(pl.BlockSpec(memory_space=pl.ANY), pl.BlockSpec(memory_space=pl.ANY)),
             scratch_shapes=scratch,
             compiler_params=pltpu.CompilerParams(collective_id=0, has_side_effects=True, vmem_limit_bytes=67043328),
         )(ridge.reshape(1, 1), target.reshape(ngroup, CH), design)
+        def emit(xi, ri, xo, ro):
+            xo[...] = xi[...]
+            ro[...] = ri[...]
+
+        x, r = pl.pallas_call(
+            emit,
+            out_shape=(jax.ShapeDtypeStruct((2 * nch, CH), F32), jax.ShapeDtypeStruct((ngroup, CH), F32)),
+        )(x, r)
         return x.reshape(-1), r.reshape(-1)
 
     return jax.shard_map(

time: 432 us -> 408 us (0.944)
  Pallas kernels: 427 us -> 406 us
    pallas_call x1, Pallas kernels: 427 us -> 405 us  [local_fit(): pl.pallas_call(kernel, out_shape=(jax.ShapeDtypeStruct((2 * nch, CH), F32...]
where the time goes in v2:
time: 408 us; the launch traced here: 407 us
  Pallas kernels  406 us (100%)
    pallas_call x1, Pallas kernels, local_fit(): pl.pallas_call(kernel, out_shape=(jax.ShapeDtypeStruct((2 * nch, CH), F32...  405 us

profile of v2, /device:TPU:0, one launch (start us, length us, event | category | flops | bytes accessed | tf_op | source)
XLA Modules:
  0.0 407.4 jit_solution(15927085719579737915)
XLA Ops:
  1.3 404.6 %shard_map.50 = (f32[8,128]{1,0:T(8,128)}, f32[128,128]{1,0:T(8,128)}) custom-call(f32[1,1]{1,0:T(1,128)} %bitcast.4.lam_ref, f32[128,128]{1,0:T(8,128)} %bitcast.5, f32[16384,512]{1,0:T(8,128)} %a_hbm.1), custom_call_target="tpu_custom_call" | custom-call | tf_op jit(solution)/shard_map/pallas_call | solution.py:480
  405.9 1.5 shard_map.51

commit v3 on v2

--- a/solution.py
+++ b/solution.py
@@ -81,10 +81,10 @@
 
 
 def kernel(
-    lam_ref, b_hbm, a_hbm, x_hbm, r_hbm,
-    b_ref, x_ref, r_ref,
+    lam_hbm, b_hbm, a_hbm, x_hbm, r_hbm,
+    lam_ref, b_ref, x_ref, x_two, r_ref,
     a_v, xr, gacc, hacc, drecv, hrecv, gall, hall, cacc, crecv, cg, pan, lp, linv, s0, s1, w0, nbuf, hpos, ybuf, pbuf, prec,
-    small_sem, load_sem, xs_sem, xr_sem, ds_sem, dr_sem, hs_sem, hr_sem, gs_sem, gr_sem, rs_sem, rr_sem, ps_sem, pr_sem, out_sem,
+    small_sem, load_sem, xs_sem, xr_sem, ds_sem, dr_sem, hs_sem, hr_sem, gs_sem, gr_sem, rs_sem, rr_sem, ps_sem, pr_sem, out_sem, xx_sem,
 ):
     rows, cols = a_v.shape
     half = rows // 2
@@ -131,6 +131,8 @@
     issue(0, ahead[0])
     b_in = pltpu.make_async_copy(b_hbm, b_ref, small_sem.at[0])
     b_in.start()
+    lam_in = pltpu.make_async_copy(lam_hbm, lam_ref, small_sem.at[2])
+    lam_in.start()
 
     gacc[...] = jnp.zeros_like(gacc)
     hacc[...] = jnp.zeros_like(hacc)
@@ -141,6 +143,7 @@
     eye = iota((CH, CH), 0) == iota((CH, CH), 1)
 
     b_in.wait()
+    lam_in.wait()
 
     mid = cols // 2
 
@@ -168,9 +171,13 @@
     def rows_of(p, n):
         return pl.ds(pl.multiple_of(p * n, n), n)
 
+    def part(p):
+        core = lax.rem(p, 2)
+        return core * (GROUPS - 1 - p // 2) + (1 - core) * (p // 2)
+
     def diag_send(off):
         p = peer(off)
-        return remote(gacc.at[rows_of(p, pr), :], drecv.at[off - 1], ds_sem.at[off - 1], dr_sem.at[off - 1], t, p)
+        return remote(gacc.at[rows_of(part(p), pr), :], drecv.at[off - 1], ds_sem.at[off - 1], dr_sem.at[off - 1], t, p)
 
     def mom_send(off):
         return remote(hacc, hrecv.at[d], hs_sem.at[off - 1], hr_sem.at[off - 1], t, peer(off))
@@ -203,40 +210,54 @@
         p = peer(off)
         return remote(cacc.at[rows_of(p, cr), :], crecv.at[k, off - 1], rs_sem.at[k, off - 1], rr_sem.at[k, off - 1], t, p)
 
-    def spread(ref, n, ssem, rsem, slot, off):
-        if slot == 7:
-            return remote(ref.at[t, rows_of(d, n), :], ref.at[t, rows_of(d, n), :], ssem.at[7], rsem.at[7], other, d)
-        plane = t if slot < 7 else other
-        return remote(
-            ref.at[plane, rows_of(d, n), :], ref.at[plane, rows_of(d, n), :], ssem.at[slot], rsem.at[slot], t, peer(off)
-        )
-
-    def arrive(ref, n, ssem, rsem, slot, off):
-        if slot == 7:
-            piece = ref.at[other, rows_of(d, n), :]
-            return remote(piece, piece, ssem.at[7], rsem.at[7], other, d)
-        src = lax.rem(d + GROUPS - off, GROUPS)
-        piece = ref.at[t if slot < 7 else other, rows_of(src, n), :]
-        return remote(piece, piece, ssem.at[slot], rsem.at[slot], t, peer(off))
-
-    def gather_start(ref, n, ssem, rsem):
-        spread(ref, n, ssem, rsem, 7, 0).start()
-        for off in range(1, GROUPS):
-            spread(ref, n, ssem, rsem, off - 1, off).start()
-
-    def gather_finish(ref, n, ssem, rsem):
-        arrive(ref, n, ssem, rsem, 7, 0).wait_recv()
-        for off in range(1, GROUPS):
-            spread(ref, n, ssem, rsem, 7 + off, off).start()
-        for off in range(1, GROUPS):
-            arrive(ref, n, ssem, rsem, off - 1, off).wait_recv()
-        for off in range(1, GROUPS):
-            arrive(ref, n, ssem, rsem, 7 + off, off).wait_recv()
-        for slot in range(7):
-            spread(ref, n, ssem, rsem, slot, slot + 1).wait_send()
-        spread(ref, n, ssem, rsem, 7, 0).wait_send()
-        for off in range(1, GROUPS):
-            spread(ref, n, ssem, rsem, 7 + off, off).wait_send()
+    def piece(ref, plane, p):
+        n = pr if ref is gall else cr
+        return ref.at[plane, rows_of(part(p) if ref is gall else p, n), :]
+
+    def spread(ref, ssem, rsem, slot, off):
+        mine = piece(ref, t if slot < 7 else other, d)
+        return remote(mine, mine, ssem.at[slot], rsem.at[slot], t, peer(off))
+
+    def arrive(ref, ssem, rsem, slot, off):
+        theirs = piece(ref, t if slot < 7 else other, lax.rem(d + GROUPS - off, GROUPS))
+        return remote(theirs, theirs, ssem.at[slot], rsem.at[slot], t, peer(off))
+
+    def across(ref, ssem, rsem, plane, act):
+        mine = piece(ref, plane, d)
+        if ref is not gall:
+            act(remote(mine, mine, ssem.at[7], rsem.at[7], other, d))
+            return
+        for j in range(nch):
+
+            @pl.when(part(d) // 2 == j)
+            def _():
+                low = gall.at[plane, rows_of(part(d), pr), : (j + 1) * CH]
+                act(remote(low, low, ssem.at[7], rsem.at[7], other, d))
+
+    def gather_start(ref, ssem, rsem):
+        across(ref, ssem, rsem, t, lambda c: c.start())
+        for off in range(1, GROUPS):
+            spread(ref, ssem, rsem, off - 1, off).start()
+
+    def gather_plane(ref, ssem, rsem):
+        across(ref, ssem, rsem, other, lambda c: c.wait_recv())
+        for off in range(1, GROUPS):
+            spread(ref, ssem, rsem, 7 + off, off).start()
+        for off in range(1, GROUPS):
+            arrive(ref, ssem, rsem, off - 1, off).wait_recv()
+
+    def gather_rest(ref, ssem, rsem):
+        for off in range(1, GROUPS):
+            arrive(ref, ssem, rsem, 7 + off, off).wait_recv()
+        for off in range(1, GROUPS):
+            spread(ref, ssem, rsem, off - 1, off).wait_send()
+        across(ref, ssem, rsem, t, lambda c: c.wait_send())
+        for off in range(1, GROUPS):
+            spread(ref, ssem, rsem, 7 + off, off).wait_send()
+
+    def gather_finish(ref, ssem, rsem):
+        gather_plane(ref, ssem, rsem)
+        gather_rest(ref, ssem, rsem)
 
     def cross_reduce(k):
         for off in range(1, GROUPS):
@@ -250,11 +271,11 @@
             cross_send(k, off).wait_send()
 
     def diag_reduce():
-        acc = gacc[rows_of(d, pr), :]
+        acc = gacc[rows_of(part(d), pr), :]
         for off in range(1, GROUPS):
             diag_send(off).wait_recv()
             acc = acc + drecv[off - 1]
-        gall[t, rows_of(d, pr), :] = acc
+        gall[t, rows_of(part(d), pr), :] = acc
         for off in range(1, GROUPS):
             mom_arrive(off).wait_recv()
         mom = hrecv[0]
@@ -291,7 +312,7 @@
         for n in range(k):
             seen = (n + 1) * wide
             lp[:, n * wide : seen] = dot(pan[:, :seen], linv[n * wide : seen, :seen], 1, 1)
-        ridge = lam_ref[0, 0]
+        ridge = lam_ref[0]
         sch = pan[:, low : low + wide] + jnp.where(iota((wide, wide), 0) == iota((wide, wide), 1), ridge, 0.0)
         if k:
             sch = sch - dot(lp[:, :low], lp[:, :low], 1, 1)
@@ -305,7 +326,7 @@
                 s0[1] = s1[:, CH:] - dot(l10, l10, 1, 1)
                 s1[:, :CH] = l10
 
-            chol_inverse(s0.at[h], w0.at[h], STEP if k < nch - 1 else LAST_STEP)
+            chol_inverse(s0.at[h], w0.at[h], STEP)
             return carry
 
         lax.fori_loop(0, 2, block, 0)
@@ -314,8 +335,6 @@
         nbuf[:CH, CH:] = jnp.zeros((CH, CH), F32)
         nbuf[CH:, :CH] = -dot(n11, dot(s1[:, :CH], n00, 1, 0), 1, 0)
         nbuf[CH:, CH:] = n11
-        if k == nch - 1:
-            return
         rhs = hpos[:, low : low + wide]
         if k:
             rhs = rhs - dot(ybuf[:, :low], lp[:, :low], 1, 1)
@@ -327,20 +346,63 @@
             linv[low : low + wide, sl] = -dot(nbuf[...], part, 1, 0)
         linv[low : low + wide, low : low + wide] = nbuf[...]
 
+    end = nch - 1
+    prev = end * wide
+    first = other
+
+    def last_rows(h, side, tc):
+        mine = pl.ds(pl.multiple_of(side * CH, CH), CH)
+        for j in range(end):
+            at = pl.ds(pl.multiple_of(j * wide + tc * CH, CH), CH)
+            pan[mine, at] += cg[end, tc, :, j * CH : (j + 1) * CH]
+        out = slice(h * CH, (h + 1) * CH)
+        for n in range(end):
+            seen = (n + 1) * wide
+            lp[out, n * wide : seen] = dot(pan[mine, :seen], linv[n * wide : seen, :seen], 1, 1)
+        blk = gall[side, end * CH :, end * CH :] + jnp.where(eye, lam_ref[0], 0.0)
+        s0[h] = blk - dot(lp[out, :], lp[out, :], 1, 1)
+
+    def last_factor(ssem, rsem):
+        gather_plane(cg.at[end], ssem, rsem)
+        last_rows(0, first, t)
+
+        def block(h, carry):
+            @pl.when(h == 1)
+            def _():
+                gather_rest(cg.at[end], ssem, rsem)
+                last_rows(1, t, first)
+                both = cg[end, first, :, end * CH :] + cg[end, t, :, end * CH :].T
+                l10 = dot(both - dot(lp[CH:, :], lp[:CH, :], 1, 1), w0[0], 1, 1)
+                s0[1] -= dot(l10, l10, 1, 1)
+                s1[:, :CH] = l10
+
+            chol_inverse(s0.at[h], w0.at[h], LAST_STEP)
+            return carry
+
+        lax.fori_loop(0, 2, block, 0)
+        n00, n11 = w0[0], w0[1]
+        nbuf[:CH, :CH] = n00
+        nbuf[:CH, CH:] = jnp.zeros((CH, CH), F32)
+        nbuf[CH:, :CH] = -dot(n11, dot(s1[:, :CH], n00, 1, 0), 1, 0)
+        nbuf[CH:, CH:] = n11
+
     for k in range(nch):
         if k:
             prepare(k)
         cross(k)
         if k == 0:
             diag_reduce()
-            gather_start(gall, pr, gs_sem.at[nch], gr_sem.at[nch])
+            gather_start(gall, gs_sem.at[nch], gr_sem.at[nch])
             mom_swap(t).start()
         cross_reduce(k)
-        gather_start(cg.at[k], cr, gs_sem.at[k], gr_sem.at[k])
+        gather_start(cg.at[k], gs_sem.at[k], gr_sem.at[k])
         issue(ahead[k], ahead[k + 1])
-        gather_finish(cg.at[k], cr, gs_sem.at[k], gr_sem.at[k])
+        if k == end:
+            last_factor(gs_sem.at[k], gr_sem.at[k])
+            break
+        gather_finish(cg.at[k], gs_sem.at[k], gr_sem.at[k])
         if k == 0:
-            gather_finish(gall, pr, gs_sem.at[nch], gr_sem.at[nch])
+            gather_finish(gall, gs_sem.at[nch], gr_sem.at[nch])
             mom_swap(other).wait_recv()
             mom_swap(t).wait_send()
             for tt in range(2):
@@ -366,14 +428,16 @@
     def down(mat, col):
         return jnp.sum(mat * col, axis=0, keepdims=True)
 
-    prev = (nch - 1) * wide
     seen = jnp.sum(lp[...] * ybuf[0:1, :], axis=1, keepdims=True)
-    rhs = hpos[0:1, prev:] - to_row(seen)
+    tail = [hpos[0:1, prev : prev + CH], hpos[0:1, prev + CH :]]
+    tail = jnp.concatenate([jnp.where(t == 1, tail[0], tail[1]), jnp.where(t == 1, tail[1], tail[0])], axis=1)
+    rhs = tail - to_row(seen)
     ycol = jnp.sum(nbuf[...] * rhs, axis=1, keepdims=True)
     last = down(nbuf[...], ycol)
     ucol = to_col(ybuf[0:1, :] - down(lp[...], to_col(last)))
     rest = [down(linv[n * wide :, n * wide : (n + 1) * wide], ucol[n * wide :]) for n in range(nch - 1)]
-    xpos = jnp.concatenate(rest + [last], axis=1)
+    turn = [jnp.where(t == 1, last[:, :CH], last[:, CH:]), jnp.where(t == 1, last[:, CH:], last[:, :CH])]
+    xpos = jnp.concatenate(rest + turn, axis=1)
     sides = [
         jnp.concatenate([xpos[0:1, (2 * j + tt) * CH : (2 * j + tt + 1) * CH] for j in range(nch)], axis=1) for tt in range(2)
     ]
@@ -381,8 +445,8 @@
         for j in range(nch):
             x_ref[tt * nch + j : tt * nch + j + 1, :] = sides[tt][:, j * CH : (j + 1) * CH]
     own = jnp.where(t == 0, sides[0], sides[1])
-    x_out = pltpu.make_async_copy(x_ref, x_hbm, small_sem.at[1])
-    x_out.start()
+    x_swap = remote(x_ref, x_two.at[0], xx_sem.at[0], xx_sem.at[1], other, d)
+    x_swap.start()
 
     def fit(m, carry):
         for g in range(8):
@@ -402,25 +466,20 @@
         sl = pl.ds(q * per, per)
         return remote(pbuf.at[sl, :], prec.at[sl, :], ps_sem.at[q], pr_sem.at[q], other, d)
 
-    def r_out(q):
-        sl = pl.ds(q * per, per)
-        return pltpu.make_async_copy(r_ref.at[sl, :], r_hbm.at[sl, :], out_sem.at[q])
-
     for q in range(parts):
         lax.fori_loop(q * per // 8, (q + 1) * per // 8, fit, 0)
         swap(q).start()
+    x_swap.wait_recv()
+    x_hbm[...] = jnp.where(t == 0, x_two[0], x_ref[...])
     for q in range(parts):
         swap(q).wait_recv()
         sl = pl.ds(q * per, per)
-        r_ref[sl, :] = b_ref[sl, :] - (pbuf[sl, :] + prec[sl, :])
-        r_out(q).start()
+        r_hbm[sl, :] = b_ref[sl, :] - (pbuf[sl, :] + prec[sl, :])
     for q in range(parts):
         swap(q).wait_send()
     for q in range(total):
         exchange(q).wait_send()
-    x_out.wait()
-    for q in range(parts):
-        r_out(q).wait()
+    x_swap.wait_send()
 
 
 def solution(mesh):
@@ -436,8 +495,10 @@
         vm = pltpu.VMEM
         dma = pltpu.SemaphoreType.DMA
         scratch = [
+            pltpu.SMEM((1,), F32),
             vm((ngroup, CH), F32),
             vm((2 * nch, CH), F32),
+            vm((2, 2 * nch, CH), F32),
             vm((ngroup, CH), F32),
             vm((rows, cols), F32),
             vm((SLOTS, half, CH), F32),
@@ -461,7 +522,7 @@
             vm((8, prev), F32),
             vm((ngroup, CH), F32),
             vm((ngroup, CH), F32),
-            dma((2,)),
+            dma((3,)),
             dma((nload,)),
             dma((nch, subs)),
             dma((nch, subs)),
@@ -476,23 +537,16 @@
             dma((4,)),
             dma((4,)),
             dma((4,)),
+            dma((2,)),
         ]
         x, r = pl.pallas_call(
             kernel,
-            out_shape=(jax.ShapeDtypeStruct((2 * nch, CH), F32), jax.ShapeDtypeStruct((ngroup, CH), F32)),
-            in_specs=[pl.BlockSpec(memory_space=pltpu.SMEM)] + [pl.BlockSpec(memory_space=pl.ANY)] * 2,
-            out_specs=(pl.BlockSpec(memory_space=pl.ANY), pl.BlockSpec(memory_space=pl.ANY)),
+            out_shape=(pltpu.VMEM((2 * nch, CH), F32), pltpu.VMEM((ngroup, CH), F32)),
+            in_specs=[pl.BlockSpec(memory_space=pl.ANY)] * 3,
+            out_specs=(pl.BlockSpec(memory_space=pltpu.VMEM), pl.BlockSpec(memory_space=pltpu.VMEM)),
             scratch_shapes=scratch,
-            compiler_params=pltpu.CompilerParams(collective_id=0, has_side_effects=True, vmem_limit_bytes=67043328),
-        )(ridge.reshape(1, 1), target.reshape(ngroup, CH), design)
-        def emit(xi, ri, xo, ro):
-            xo[...] = xi[...]
-            ro[...] = ri[...]
-
-        x, r = pl.pallas_call(
-            emit,
-            out_shape=(jax.ShapeDtypeStruct((2 * nch, CH), F32), jax.ShapeDtypeStruct((ngroup, CH), F32)),
-        )(x, r)
+            compiler_params=pltpu.CompilerParams(collective_id=0, has_side_effects=True, vmem_limit_bytes=66781184),
+        )(ridge.reshape(1), target.reshape(ngroup, CH), design)
         return x.reshape(-1), r.reshape(-1)
 
     return jax.shard_map(

time: 408 us -> 406 us (level)
    pallas_call x2 -> x1, Pallas kernels: 406 us -> 403 us  [local_fit(): pl.pallas_call(kernel, out_shape=(pltpu.VMEM((2 * nch, CH), F32), pltpu.V...]
where the time goes in v3:
time: 406 us; the launch traced here: 405 us
  Pallas kernels  403 us (99%)
    pallas_call x1, Pallas kernels, local_fit(): pl.pallas_call(kernel, out_shape=(pltpu.VMEM((2 * nch, CH), F32), pltpu.V...  403 us

profile of v3, /device:TPU:0, one launch (start us, length us, event | category | flops | bytes accessed | tf_op | source)
XLA Modules:
  0.0 405.4 jit_solution(15115131972841649827)
XLA Ops:
  1.3 402.9 %shard_map.50 = (f32[8,128]{1,0:T(8,128)S(1)}, f32[128,128]{1,0:T(8,128)S(1)}) custom-call(f32[1]{0:T(128)} %bitcast.4.lam_hbm, f32[128,128]{1,0:T(8,128)} %bitcast.7, f32[16384,512]{1,0:T(8,128)} %a_hbm.1), custom_call_target="tpu_custom_call" | custom-call | tf_op jit(solution)/shard_map/pallas_call | solution.py:542
  404.2 0.6 copy.7
  404.8 0.6 copy.8
